TPU v7x, 32 devices: a whole 2x2x4 slice. The times are simulated.
32 devices in a mesh: panel: 4 (over z), rows: 8 (over y, x, core).
Axes of the slice: x: 2, y: 2, z: 4, core: 2. Of those that a mesh axis runs over, the one named last changes fastest.
Arguments:
- rhs_diag: bfloat16 [4, 4096, 128], P(None, 'rows'), may hold values from -6 to 6
- rhs_tall: bfloat16 [4, 4096, 128], P('panel', 'rows'), may hold values from -6 to 6
- diag_inverse: bfloat16 [4, 1024, 1024], P('panel'), may hold values from -0.1875 to 0.1875
- coupling: bfloat16 [4, 4096, 1024], P('panel', 'rows'), may hold values from -0.09375 to 0.09375
- tall_blocks: bfloat16 [4, 32, 128, 1024], P('panel', 'rows'), may hold values from -0.125 to 0.125
- sparsity: int32 [32, 4], P('rows', 'panel'), may hold values 0 or 1
Outputs:
- solution: float32 [4, 4, 1024, 128], P('panel', None, 'rows')
- tall_residual: float32 [4, 4096, 128], P('panel', 'rows')
All inputs are finite; a program needn't handle non-finite values. No bound on the sum of `sparsity` on one device may be relied on, other than what follows from the above.
Results may differ from a plain program's by a relative error of at most 0.0085.
Values may be sent and summed in bfloat16 or wider, within the bound.
A program may use at most 64 MiB of HBM per device.

v0:
```python
import jax
import jax.numpy as jnp
from jax import lax
from jax.sharding import PartitionSpec as P


def shifted(block, axis, distance):
    devices = range(lax.axis_size(axis))
    route = [(i - distance, i) for i in devices if i - distance in devices]
    return lax.ppermute(block, axis, route)


def per_device(rhs_diag, rhs_tall, diag_inverse, coupling, tall_blocks, sparsity):
    panel_index = lax.axis_index("panel")
    rows_index = lax.axis_index("rows")
    panel_count = lax.axis_size("panel")
    rows_count = lax.axis_size("rows")
    batches, rows_here, columns = rhs_diag.shape
    panel_width = diag_inverse.shape[1]
    slice_rows = panel_width // rows_count
    blocks_here = tall_blocks.shape[1]
    block_rows = tall_blocks.shape[2]
    tall_rows = blocks_here * block_rows
    rows_panel = rows_index * rows_here // panel_width
    offset = jnp.clip(
        rows_index * rows_here - panel_index * panel_width, 0, panel_width - rows_here
    )
    inverse_cols = lax.dynamic_slice_in_dim(diag_inverse[0], offset, rows_here, 1)
    owner = rows_panel == panel_index
    is_later = rows_panel > panel_index
    coupling_here = coupling[0]
    tall_matrix = tall_blocks[0].reshape(tall_rows, panel_width)
    block_mask = jnp.repeat(sparsity[:, 0].astype(jnp.float32), block_rows)[:, None]

    def advance(tick_number, state_now):
        incoming, solutions, stored = state_now
        batch_now = tick_number - panel_index
        active = (batch_now >= 0) & (batch_now < batches)
        batch_safe = jnp.clip(batch_now, 0, batches - 1)
        rhs_now = lax.dynamic_index_in_dim(rhs_diag, batch_safe, 0, keepdims=False).astype(
            jnp.float32
        )
        reduced = (rhs_now - incoming).astype(jnp.bfloat16)
        partial_value = jnp.dot(inverse_cols, reduced, preferred_element_type=jnp.float32)
        partial_value = jnp.where(owner, partial_value, jnp.float32(0.0))
        own_rows = lax.psum_scatter(partial_value, "rows", scatter_dimension=0, tiled=True)
        solved = lax.all_gather(own_rows.astype(jnp.bfloat16), "rows", axis=0, tiled=True)
        previous = lax.dynamic_index_in_dim(solutions, batch_safe, 0, keepdims=False)
        solutions = lax.dynamic_update_index_in_dim(
            solutions, jnp.where(active, own_rows, previous), batch_safe, 0
        )
        update = jnp.dot(coupling_here, solved, preferred_element_type=jnp.float32)
        outgoing = incoming + jnp.where(is_later, update, jnp.float32(0.0))
        earlier = lax.dynamic_index_in_dim(stored, batch_safe, 0, keepdims=False)
        stored = lax.dynamic_update_index_in_dim(
            stored, jnp.where(active, solved, earlier), batch_safe, 0
        )
        incoming = shifted(outgoing, "panel", 1)
        return (incoming, solutions, stored)

    stored = jnp.zeros((batches, panel_width, columns), jnp.bfloat16)
    initial = (
        jnp.zeros((rows_here, columns), jnp.float32),
        jnp.zeros((batches, slice_rows, columns), jnp.float32),
        stored,
    )
    tick_count = batches + panel_count - 1
    incoming, solutions, stored = lax.fori_loop(0, tick_count, advance, initial)
    tall_terms = (
        jnp.einsum("rw,bws->brs", tall_matrix, stored, preferred_element_type=jnp.float32)
        * block_mask
    )
    summed = lax.psum_scatter(tall_terms, "panel", scatter_dimension=0, tiled=True)
    tall_residual = rhs_tall.astype(jnp.float32) - summed
    return (solutions[None], tall_residual)


def solution(mesh):
    placed = (
        P(None, "rows", None),
        P("panel", "rows", None),
        P("panel", None, None),
        P("panel", "rows", None),
        P("panel", "rows", None, None),
        P("rows", "panel"),
    )
    return jax.shard_map(
        per_device,
        mesh=mesh,
        in_specs=placed,
        out_specs=(P("panel", None, "rows", None), P("panel", "rows", None)),
        check_vma=False,
    )
```

profile of v0, /device:TPU:0, one launch (start us, length us, event | category | flops | bytes accessed | tf_op | source)
XLA Modules:
  0.0 485.0 jit_solution(7875205696429187372)
XLA Ops:
  11.6 1.1 broadcast_in_dim.49
  12.7 431.4 %while.17 = (s32[]{:T(128)}, f32[512,128]{0,1:T(8,128)}, f32[4,128,128]{2,1,0:T(8,128)}, bf16[4,1024,128]{1,2,0:T(8,128)(2,1)}, pred[]{:T(512)}, /*index=5*/pred...) while((s32[]{:T(128)}, f32[512,128]{0,1:T(8,128)}, ...), condition=%wide.region_2.3_spmd, body=%wide.region_0.2_spmd.sunk | while | flops 269058048 | bytes 9503014 | solution.py:68
  13.7 2.2 fusion.24
  16.9 1.7 constant_dynamic-slice_fusion.8
  18.6 34.8 %reduce-scatter.5.cloned.1.call-done = f32[128,128]{0,1:T(8,128)} async-done(((f32[1024,128]{0,1:T(8,128)}), f32[128,128]{0,1:T(8,128)}) %reduce-scatter.5.cloned.1.call-update) | async-done | bytes 65552 | tf_op jit(solution)/shard_map/while/body/eval_jaxpr/reduce_scatter | solution.py:46
  53.4 0.9 fusion.25
  54.3 9.3 %all_gather.8 = bf16[1024,128]{0,1:T(8,128)(2,1)S(1)} all-gather(bf16[128,128]{0,1:T(8,128)(2,1)S(1)} %get-tuple-element.271), channel_id=1, replica_groups=mesh['panel'=4,'rows'=8] {'rows'}, dimensions={0}, use_global_device_ids=true | all-gather | bytes 294912 | tf_op jit(solution)/shard_map/while/body/eval_jaxpr/all_gather | solution.py:47
  63.6 2.5 fusion.26
  66.1 4.1 collective-permute-start
  70.9 1.7 bitcast_dynamic-update-slice_fusion.2
  72.6 3.2 collective-permute-done
  76.9 2.2 fusion.24
  80.1 1.7 constant_dynamic-slice_fusion.8
  81.8 33.1 %reduce-scatter.5.cloned.1.call-done = f32[128,128]{0,1:T(8,128)} async-done(((f32[1024,128]{0,1:T(8,128)}), f32[128,128]{0,1:T(8,128)}) %reduce-scatter.5.cloned.1.call-update) | async-done | bytes 65552 | tf_op jit(solution)/shard_map/while/body/eval_jaxpr/reduce_scatter | solution.py:46
  115.8 9.3 %all_gather.8 = bf16[1024,128]{0,1:T(8,128)(2,1)S(1)} all-gather(bf16[128,128]{0,1:T(8,128)(2,1)S(1)} %get-tuple-element.271), channel_id=1, replica_groups=mesh['panel'=4,'rows'=8] {'rows'}, dimensions={0}, use_global_device_ids=true | all-gather | bytes 294912 | tf_op jit(solution)/shard_map/while/body/eval_jaxpr/all_gather | solution.py:47
  125.2 2.5 fusion.26
  127.6 4.1 collective-permute-start
  132.4 1.7 bitcast_dynamic-update-slice_fusion.2
  134.1 3.2 collective-permute-done
  138.4 2.2 fusion.24
  141.6 1.7 constant_dynamic-slice_fusion.8
  143.3 33.1 %reduce-scatter.5.cloned.1.call-done = f32[128,128]{0,1:T(8,128)} async-done(((f32[1024,128]{0,1:T(8,128)}), f32[128,128]{0,1:T(8,128)}) %reduce-scatter.5.cloned.1.call-update) | async-done | bytes 65552 | tf_op jit(solution)/shard_map/while/body/eval_jaxpr/reduce_scatter | solution.py:46
  177.3 9.3 %all_gather.8 = bf16[1024,128]{0,1:T(8,128)(2,1)S(1)} all-gather(bf16[128,128]{0,1:T(8,128)(2,1)S(1)} %get-tuple-element.271), channel_id=1, replica_groups=mesh['panel'=4,'rows'=8] {'rows'}, dimensions={0}, use_global_device_ids=true | all-gather | bytes 294912 | tf_op jit(solution)/shard_map/while/body/eval_jaxpr/all_gather | solution.py:47
  186.7 2.5 fusion.26
  189.1 4.1 collective-permute-start
  193.9 1.7 bitcast_dynamic-update-slice_fusion.2
  195.6 3.3 collective-permute-done
  199.9 2.2 fusion.24
  203.2 1.7 constant_dynamic-slice_fusion.8
  204.8 32.8 %reduce-scatter.5.cloned.1.call-done = f32[128,128]{0,1:T(8,128)} async-done(((f32[1024,128]{0,1:T(8,128)}), f32[128,128]{0,1:T(8,128)}) %reduce-scatter.5.cloned.1.call-update) | async-done | bytes 65552 | tf_op jit(solution)/shard_map/while/body/eval_jaxpr/reduce_scatter | solution.py:46
  237.6 0.9 fusion.25
  238.5 9.3 %all_gather.8 = bf16[1024,128]{0,1:T(8,128)(2,1)S(1)} all-gather(bf16[128,128]{0,1:T(8,128)(2,1)S(1)} %get-tuple-element.271), channel_id=1, replica_groups=mesh['panel'=4,'rows'=8] {'rows'}, dimensions={0}, use_global_device_ids=true | all-gather | bytes 294912 | tf_op jit(solution)/shard_map/while/body/eval_jaxpr/all_gather | solution.py:47
  247.9 2.5 fusion.26
  250.3 4.1 collective-permute-start
  255.1 1.7 bitcast_dynamic-update-slice_fusion.2
  256.9 3.2 collective-permute-done
  261.1 2.2 fusion.24
  264.4 1.7 constant_dynamic-slice_fusion.8
  266.0 32.8 %reduce-scatter.5.cloned.1.call-done = f32[128,128]{0,1:T(8,128)} async-done(((f32[1024,128]{0,1:T(8,128)}), f32[128,128]{0,1:T(8,128)}) %reduce-scatter.5.cloned.1.call-update) | async-done | bytes 65552 | tf_op jit(solution)/shard_map/while/body/eval_jaxpr/reduce_scatter | solution.py:46
  298.8 0.9 fusion.25
  299.7 9.3 %all_gather.8 = bf16[1024,128]{0,1:T(8,128)(2,1)S(1)} all-gather(bf16[128,128]{0,1:T(8,128)(2,1)S(1)} %get-tuple-element.271), channel_id=1, replica_groups=mesh['panel'=4,'rows'=8] {'rows'}, dimensions={0}, use_global_device_ids=true | all-gather | bytes 294912 | tf_op jit(solution)/shard_map/while/body/eval_jaxpr/all_gather | solution.py:47
  309.1 2.5 fusion.26
  311.5 4.1 collective-permute-start
  316.3 1.7 bitcast_dynamic-update-slice_fusion.2
  318.1 3.2 collective-permute-done
  322.3 2.2 fusion.24
  325.6 1.7 constant_dynamic-slice_fusion.8
  327.2 32.8 %reduce-scatter.5.cloned.1.call-done = f32[128,128]{0,1:T(8,128)} async-done(((f32[1024,128]{0,1:T(8,128)}), f32[128,128]{0,1:T(8,128)}) %reduce-scatter.5.cloned.1.call-update) | async-done | bytes 65552 | tf_op jit(solution)/shard_map/while/body/eval_jaxpr/reduce_scatter | solution.py:46
  360.9 9.3 %all_gather.8 = bf16[1024,128]{0,1:T(8,128)(2,1)S(1)} all-gather(bf16[128,128]{0,1:T(8,128)(2,1)S(1)} %get-tuple-element.271), channel_id=1, replica_groups=mesh['panel'=4,'rows'=8] {'rows'}, dimensions={0}, use_global_device_ids=true | all-gather | bytes 294912 | tf_op jit(solution)/shard_map/while/body/eval_jaxpr/all_gather | solution.py:47
  370.3 2.5 fusion.26
  372.7 4.1 collective-permute-start
  377.5 1.7 bitcast_dynamic-update-slice_fusion.2
  379.3 3.2 collective-permute-done
  383.5 2.2 fusion.24
  386.8 1.7 constant_dynamic-slice_fusion.8
  388.4 33.1 %reduce-scatter.5.cloned.1.call-done = f32[128,128]{0,1:T(8,128)} async-done(((f32[1024,128]{0,1:T(8,128)}), f32[128,128]{0,1:T(8,128)}) %reduce-scatter.5.cloned.1.call-update) | async-done | bytes 65552 | tf_op jit(solution)/shard_map/while/body/eval_jaxpr/reduce_scatter | solution.py:46
  422.5 9.3 %all_gather.8 = bf16[1024,128]{0,1:T(8,128)(2,1)S(1)} all-gather(bf16[128,128]{0,1:T(8,128)(2,1)S(1)} %get-tuple-element.271), channel_id=1, replica_groups=mesh['panel'=4,'rows'=8] {'rows'}, dimensions={0}, use_global_device_ids=true | all-gather | bytes 294912 | tf_op jit(solution)/shard_map/while/body/eval_jaxpr/all_gather | solution.py:47
  431.8 2.5 fusion.26
  434.3 4.1 collective-permute-start
  439.1 1.7 bitcast_dynamic-update-slice_fusion.2
  440.8 3.2 collective-permute-done
  444.0 3.3 fusion.7
  447.5 28.2 %reduce-scatter.3.cloned.1.call-done = f32[1,512,128]{1,2,0:T(8,128)} async-done(((f32[4,512,128]{1,2,0:T(8,128)}), f32[1,512,128]{1,2,0:T(8,128)}) %reduce-scatter.3.cloned.1.call-update) | async-done | bytes 262160 | tf_op jit(solution)/shard_map/reduce_scatter | solution.py:73
  475.8 1.0 convert_subtract_fusion.1
  (73 shorter events, 27.2 us)
Async XLA Ops:
  8.0 1.6 copy-start
  12.7 40.7 %reduce-scatter.5.cloned.1.call-start = ((), (), s32[]{:S(2)}) async-start(), calls=%async_computation.3 | async-start | bytes 589824 | tf_op jit(solution)/shard_map/while/body/eval_jaxpr/reduce_scatter | solution.py:46
  66.1 9.8 %collective-permute-start = (f32[512,128]{0,1:T(8,128)}, f32[512,128]{0,1:T(8,128)}, u32[]{:S(2)}, u32[]{:S(2)}) collective-permute-start(f32[512,128]{0,1:T(8,128)} %fusion.26), channel_id=1, source_target_pairs={{0,8},{8,16},{16,24},{1,9},{9,17},{17,25},{2,10},{10,18},{18,26},{... | collective-permute-start | bytes 786440 | tf_op jit(solution)/shard_map/while/body/eval_jaxpr/ppermute | solution.py:10
  75.9 39.0 %reduce-scatter.5.cloned.1.call-start = ((), (), s32[]{:S(2)}) async-start(), calls=%async_computation.3 | async-start | bytes 589824 | tf_op jit(solution)/shard_map/while/body/eval_jaxpr/reduce_scatter | solution.py:46
  127.6 9.8 %collective-permute-start = (f32[512,128]{0,1:T(8,128)}, f32[512,128]{0,1:T(8,128)}, u32[]{:S(2)}, u32[]{:S(2)}) collective-permute-start(f32[512,128]{0,1:T(8,128)} %fusion.26), channel_id=1, source_target_pairs={{0,8},{8,16},{16,24},{1,9},{9,17},{17,25},{2,10},{10,18},{18,26},{... | collective-permute-start | bytes 786440 | tf_op jit(solution)/shard_map/while/body/eval_jaxpr/ppermute | solution.py:10
  137.4 39.0 %reduce-scatter.5.cloned.1.call-start = ((), (), s32[]{:S(2)}) async-start(), calls=%async_computation.3 | async-start | bytes 589824 | tf_op jit(solution)/shard_map/while/body/eval_jaxpr/reduce_scatter | solution.py:46
  189.1 9.8 %collective-permute-start = (f32[512,128]{0,1:T(8,128)}, f32[512,128]{0,1:T(8,128)}, u32[]{:S(2)}, u32[]{:S(2)}) collective-permute-start(f32[512,128]{0,1:T(8,128)} %fusion.26), channel_id=1, source_target_pairs={{0,8},{8,16},{16,24},{1,9},{9,17},{17,25},{2,10},{10,18},{18,26},{... | collective-permute-start | bytes 786440 | tf_op jit(solution)/shard_map/while/body/eval_jaxpr/ppermute | solution.py:10
  198.9 38.7 %reduce-scatter.5.cloned.1.call-start = ((), (), s32[]{:S(2)}) async-start(), calls=%async_computation.3 | async-start | bytes 589824 | tf_op jit(solution)/shard_map/while/body/eval_jaxpr/reduce_scatter | solution.py:46
  250.3 9.8 %collective-permute-start = (f32[512,128]{0,1:T(8,128)}, f32[512,128]{0,1:T(8,128)}, u32[]{:S(2)}, u32[]{:S(2)}) collective-permute-start(f32[512,128]{0,1:T(8,128)} %fusion.26), channel_id=1, source_target_pairs={{0,8},{8,16},{16,24},{1,9},{9,17},{17,25},{2,10},{10,18},{18,26},{... | collective-permute-start | bytes 786440 | tf_op jit(solution)/shard_map/while/body/eval_jaxpr/ppermute | solution.py:10
  260.1 38.7 %reduce-scatter.5.cloned.1.call-start = ((), (), s32[]{:S(2)}) async-start(), calls=%async_computation.3 | async-start | bytes 589824 | tf_op jit(solution)/shard_map/while/body/eval_jaxpr/reduce_scatter | solution.py:46
  311.5 9.8 %collective-permute-start = (f32[512,128]{0,1:T(8,128)}, f32[512,128]{0,1:T(8,128)}, u32[]{:S(2)}, u32[]{:S(2)}) collective-permute-start(f32[512,128]{0,1:T(8,128)} %fusion.26), channel_id=1, source_target_pairs={{0,8},{8,16},{16,24},{1,9},{9,17},{17,25},{2,10},{10,18},{18,26},{... | collective-permute-start | bytes 786440 | tf_op jit(solution)/shard_map/while/body/eval_jaxpr/ppermute | solution.py:10
  321.3 38.7 %reduce-scatter.5.cloned.1.call-start = ((), (), s32[]{:S(2)}) async-start(), calls=%async_computation.3 | async-start | bytes 589824 | tf_op jit(solution)/shard_map/while/body/eval_jaxpr/reduce_scatter | solution.py:46
  372.7 9.8 %collective-permute-start = (f32[512,128]{0,1:T(8,128)}, f32[512,128]{0,1:T(8,128)}, u32[]{:S(2)}, u32[]{:S(2)}) collective-permute-start(f32[512,128]{0,1:T(8,128)} %fusion.26), channel_id=1, source_target_pairs={{0,8},{8,16},{16,24},{1,9},{9,17},{17,25},{2,10},{10,18},{18,26},{... | collective-permute-start | bytes 786440 | tf_op jit(solution)/shard_map/while/body/eval_jaxpr/ppermute | solution.py:10
  382.5 39.0 %reduce-scatter.5.cloned.1.call-start = ((), (), s32[]{:S(2)}) async-start(), calls=%async_computation.3 | async-start | bytes 589824 | tf_op jit(solution)/shard_map/while/body/eval_jaxpr/reduce_scatter | solution.py:46
  434.3 9.8 %collective-permute-start = (f32[512,128]{0,1:T(8,128)}, f32[512,128]{0,1:T(8,128)}, u32[]{:S(2)}, u32[]{:S(2)}) collective-permute-start(f32[512,128]{0,1:T(8,128)} %fusion.26), channel_id=1, source_target_pairs={{0,8},{8,16},{16,24},{1,9},{9,17},{17,25},{2,10},{10,18},{18,26},{... | collective-permute-start | bytes 786440 | tf_op jit(solution)/shard_map/while/body/eval_jaxpr/ppermute | solution.py:10
  444.0 31.7 %reduce-scatter.3.cloned.1.call-start = ((), (), s32[]{:S(2)}) async-start(), calls=%async_computation.2 | async-start | bytes 1310720 | tf_op jit(solution)/shard_map/reduce_scatter | solution.py:73
  444.0 3.4 copy-start.1
Sparse Core Ops, SparseCore 0:
  16.5 36.8 reduce-scatter.4
  79.7 35.1 reduce-scatter.4
  141.2 35.1 reduce-scatter.4
  202.5 35.1 reduce-scatter.4
  263.7 35.1 reduce-scatter.4
  324.9 35.1 reduce-scatter.4
  386.4 35.1 reduce-scatter.4
Sparse Core Ops, SparseCore 1:
  447.5 28.2 reduce-scatter.2
where the time goes:
time: 487 us; the launch traced here: 485 us
  waiting for transfers between devices  283 us (58%)
  blocking collectives  65.4 us (13%)
  matrix products  36.2 us (7%)
  local copies, waits for them, and re-layouts  35.3 us (7%)
  starting transfers between devices  28.5 us (6%)
  other arithmetic  20.3 us (4%)
  between operations  15.5 us (3%)
    reduce_scatter x7, waiting for transfers between devices, advance(): lax.psum_scatter(partial_value, 'rows', scatter_dimension=0, tiled=True)  232 us
    all_gather x7, blocking collectives, advance(): lax.all_gather(own_rows.astype(jnp.bfloat16), 'rows', axis=0, tiled=True)  65.4 us
    ppermute x7, starting transfers between devices, shifted(): return lax.ppermute(block, axis, route)  28.5 us
    reduce_scatter x1, waiting for transfers between devices, per_device(): lax.psum_scatter(tall_terms, 'panel', scatter_dimension=0, tiled=True)  28.2 us
    ppermute x7, waiting for transfers between devices, shifted(): return lax.ppermute(block, axis, route)  22.7 us
    dot_general x7, matrix products, advance(): update = jnp.dot(coupling_here, solved, preferred_element_type=jnp.float32)  17.2 us
    dot_general x7, matrix products, advance(): jnp.dot(inverse_cols, reduced, preferred_element_type=jnp.float32)  15.6 us
    dynamic_update_slice x7, other arithmetic, advance(): lax.dynamic_update_index_in_dim(stored, jnp.where(active, solved, earlier...  12 us
  transfers between devices with their start and end apart: 15, of which 15 were waited for; matrix products, arithmetic and copies ran while one was open for 7% of the time, Pallas kernels for 0%

commit v1 on v0

--- a/solution.py
+++ b/solution.py
@@ -44,7 +44,17 @@
         partial_value = jnp.dot(inverse_cols, reduced, preferred_element_type=jnp.float32)
         partial_value = jnp.where(owner, partial_value, jnp.float32(0.0))
         own_rows = lax.psum_scatter(partial_value, "rows", scatter_dimension=0, tiled=True)
-        solved = lax.all_gather(own_rows.astype(jnp.bfloat16), "rows", axis=0, tiled=True)
+        shard = own_rows.astype(jnp.bfloat16)
+        size, index, rows = (lax.axis_size("rows"), lax.axis_index("rows"), shard.shape[0])
+        right = [(i_2, (i_2 + 1) % size) for i_2 in range(size)]
+        out = jnp.zeros((*shard.shape[:0], size * rows, *shard.shape[0 + 1 :]), shard.dtype)
+        current = shard
+        for lap in range(size):
+            source = (index - lap) % size
+            out = lax.dynamic_update_slice_in_dim(out, current, source * rows, axis=0)
+            if lap < size - 1:
+                current = lax.ppermute(current, "rows", right)
+        solved = out
         previous = lax.dynamic_index_in_dim(solutions, batch_safe, 0, keepdims=False)
         solutions = lax.dynamic_update_index_in_dim(
             solutions, jnp.where(active, own_rows, previous), batch_safe, 0

time: 487 us -> 616 us (1.26)
  waiting for transfers between devices: 283 us -> 473 us
  blocking collectives: 65.4 us -> 0 us
    ppermute x0 -> x49, waiting for transfers between devices: none -> 201 us  [advance(): current = lax.ppermute(current, 'rows', right)]
    all_gather x7 -> x0, blocking collectives: 65.4 us -> none  [advance(): lax.all_gather(own_rows.astype(jnp.bfloat16), 'rows', axis=0, tiled=True)]
    ppermute x7, waiting for transfers between devices: 22.7 us -> 12.3 us  [shifted(): return lax.ppermute(block, axis, route)]
    dynamic_update_slice x0 -> x7, other arithmetic: none -> 10.3 us  [advance(): out = lax.dynamic_update_slice_in_dim(out, current, source * rows, axis=0)]
    dynamic_update_slice x7, other arithmetic: 12 us -> 5.42 us  [advance(): lax.dynamic_update_index_in_dim(stored, jnp.where(active, solved, earlier...]
  transfers between devices with their start and end apart: 15 -> 64, of which waited for: 15 -> 64; matrix products, arithmetic and copies ran while one was open for 7% -> 6% of each run, Pallas kernels for 0% -> 0%
where the time goes in v1:
time: 616 us; the launch traced here: 613 us
  waiting for transfers between devices  473 us (77%)
  local copies, waits for them, and re-layouts  41.4 us (7%)
  matrix products  31.4 us (5%)
  starting transfers between devices  28.9 us (5%)
  other arithmetic  20.9 us (3%)
  between operations  15.5 us (3%)
    reduce_scatter x7, waiting for transfers between devices, advance(): lax.psum_scatter(partial_value, 'rows', scatter_dimension=0, tiled=True)  231 us
    ppermute x49, waiting for transfers between devices, advance(): current = lax.ppermute(current, 'rows', right)  201 us
    ppermute x7, starting transfers between devices, shifted(): return lax.ppermute(block, axis, route)  28.8 us
    reduce_scatter x1, waiting for transfers between devices, per_device(): lax.psum_scatter(tall_terms, 'panel', scatter_dimension=0, tiled=True)  28.3 us
    dot_general x7, matrix products, advance(): jnp.dot(inverse_cols, reduced, preferred_element_type=jnp.float32)  15.8 us
  transfers between devices with their start and end apart: 64, of which 64 were waited for; matrix products, arithmetic and copies ran while one was open for 6% of the time, Pallas kernels for 0%

profile of v1, /device:TPU:0, one launch (start us, length us, event | category | flops | bytes accessed | tf_op | source)
XLA Modules:
  0.0 613.5 jit_solution(10291913815944575267)
XLA Ops:
  12.7 559.8 %while.19 = (s32[]{:T(128)}, f32[512,128]{0,1:T(8,128)}, f32[4,128,128]{2,1,0:T(8,128)}, bf16[4,1024,128]{1,2,0:T(8,128)(2,1)}, pred[]{:T(512)}, /*index=5*/pred...) while((s32[]{:T(128)}, f32[512,128]{0,1:T(8,128)}, ...), condition=%wide.region_2.3_spmd, body=%wide.region_0.2_spmd.sunk | while | flops 269058048 | bytes 11995172 | solution.py:78
  18.8 34.6 %reduce-scatter.5.cloned.1.call-done = f32[128,128]{0,1:T(8,128)} async-done(((f32[1024,128]{0,1:T(8,128)}), f32[128,128]{0,1:T(8,128)}) %reduce-scatter.5.cloned.1.call-update) | async-done | bytes 65552 | tf_op jit(solution)/shard_map/while/body/eval_jaxpr/reduce_scatter | solution.py:46
  55.9 3.6 collective-permute-done
  60.2 3.7 collective-permute-done.1
  63.9 4.2 collective-permute-done.2
  68.2 4.2 collective-permute-done.3
  72.4 4.2 collective-permute-done.4
  76.6 4.2 collective-permute-done.5
  80.9 4.2 collective-permute-done.6
  86.9 4.1 collective-permute-start.7
  100.3 33.0 %reduce-scatter.5.cloned.1.call-done = f32[128,128]{0,1:T(8,128)} async-done(((f32[1024,128]{0,1:T(8,128)}), f32[128,128]{0,1:T(8,128)}) %reduce-scatter.5.cloned.1.call-update) | async-done | bytes 65552 | tf_op jit(solution)/shard_map/while/body/eval_jaxpr/reduce_scatter | solution.py:46
  135.7 3.6 collective-permute-done
  140.1 3.7 collective-permute-done.1
  143.8 4.2 collective-permute-done.2
  148.0 4.2 collective-permute-done.3
  152.3 4.2 collective-permute-done.4
  156.5 4.2 collective-permute-done.5
  160.7 4.2 collective-permute-done.6
  166.7 4.1 collective-permute-start.7
  180.2 33.0 %reduce-scatter.5.cloned.1.call-done = f32[128,128]{0,1:T(8,128)} async-done(((f32[1024,128]{0,1:T(8,128)}), f32[128,128]{0,1:T(8,128)}) %reduce-scatter.5.cloned.1.call-update) | async-done | bytes 65552 | tf_op jit(solution)/shard_map/while/body/eval_jaxpr/reduce_scatter | solution.py:46
  215.6 3.6 collective-permute-done
  220.0 3.7 collective-permute-done.1
  223.6 4.2 collective-permute-done.2
  227.9 4.2 collective-permute-done.3
  232.1 4.2 collective-permute-done.4
  236.4 4.2 collective-permute-done.5
  240.6 4.2 collective-permute-done.6
  246.6 4.1 collective-permute-start.7
  260.0 32.6 %reduce-scatter.5.cloned.1.call-done = f32[128,128]{0,1:T(8,128)} async-done(((f32[1024,128]{0,1:T(8,128)}), f32[128,128]{0,1:T(8,128)}) %reduce-scatter.5.cloned.1.call-update) | async-done | bytes 65552 | tf_op jit(solution)/shard_map/while/body/eval_jaxpr/reduce_scatter | solution.py:46
  299.5 3.7 collective-permute-done.1
  303.2 4.2 collective-permute-done.2
  307.4 4.2 collective-permute-done.3
  311.7 4.2 collective-permute-done.4
  315.9 4.2 collective-permute-done.5
  320.2 4.2 collective-permute-done.6
  326.1 4.1 collective-permute-start.7
  339.6 32.6 %reduce-scatter.5.cloned.1.call-done = f32[128,128]{0,1:T(8,128)} async-done(((f32[1024,128]{0,1:T(8,128)}), f32[128,128]{0,1:T(8,128)}) %reduce-scatter.5.cloned.1.call-update) | async-done | bytes 65552 | tf_op jit(solution)/shard_map/while/body/eval_jaxpr/reduce_scatter | solution.py:46
  373.8 4.4 collective-permute-done
  379.0 3.7 collective-permute-done.1
  382.7 4.2 collective-permute-done.2
  387.0 4.2 collective-permute-done.3
  391.2 4.2 collective-permute-done.4
  395.5 4.2 collective-permute-done.5
  399.7 4.2 collective-permute-done.6
  405.7 4.1 collective-permute-start.7
  419.1 32.7 %reduce-scatter.5.cloned.1.call-done = f32[128,128]{0,1:T(8,128)} async-done(((f32[1024,128]{0,1:T(8,128)}), f32[128,128]{0,1:T(8,128)}) %reduce-scatter.5.cloned.1.call-update) | async-done | bytes 65552 | tf_op jit(solution)/shard_map/while/body/eval_jaxpr/reduce_scatter | solution.py:46
  453.4 4.4 collective-permute-done
  458.6 3.7 collective-permute-done.1
  462.3 4.2 collective-permute-done.2
  466.6 4.2 collective-permute-done.3
  470.8 4.2 collective-permute-done.4
  475.0 4.2 collective-permute-done.5
  479.3 4.2 collective-permute-done.6
  485.3 4.1 collective-permute-start.7
  498.7 33.0 %reduce-scatter.5.cloned.1.call-done = f32[128,128]{0,1:T(8,128)} async-done(((f32[1024,128]{0,1:T(8,128)}), f32[128,128]{0,1:T(8,128)}) %reduce-scatter.5.cloned.1.call-update) | async-done | bytes 65552 | tf_op jit(solution)/shard_map/while/body/eval_jaxpr/reduce_scatter | solution.py:46
  533.3 4.4 collective-permute-done
  538.5 3.7 collective-permute-done.1
  542.2 4.2 collective-permute-done.2
  546.4 4.2 collective-permute-done.3
  550.7 4.2 collective-permute-done.4
  554.9 4.2 collective-permute-done.5
  559.2 4.2 collective-permute-done.6
  565.2 4.1 collective-permute-start.7
  575.9 28.3 %reduce-scatter.3.cloned.1.call-done = f32[1,512,128]{1,2,0:T(8,128)} async-done(((f32[4,512,128]{1,2,0:T(8,128)}), f32[1,512,128]{1,2,0:T(8,128)}) %reduce-scatter.3.cloned.1.call-update) | async-done | bytes 262160 | tf_op jit(solution)/shard_map/reduce_scatter | solution.py:83
  (241 shorter events, 109.9 us)
Async XLA Ops:
  12.7 40.7 %reduce-scatter.5.cloned.1.call-start = ((), (), s32[]{:S(2)}) async-start(), calls=%async_computation.3 | async-start | bytes 589824 | tf_op jit(solution)/shard_map/while/body/eval_jaxpr/reduce_scatter | solution.py:46
  54.9 4.6 collective-permute-start
  59.4 4.4 collective-permute-start.1
  63.9 4.2 collective-permute-start.2
  68.1 4.2 collective-permute-start.3
  72.4 4.2 collective-permute-start.4
  76.6 4.2 collective-permute-start.5
  80.9 4.2 collective-permute-start.6
  86.9 7.3 %collective-permute-start.7 = (f32[512,128]{0,1:T(8,128)S(1)}, f32[512,128]{0,1:T(8,128)}, u32[]{:S(2)}, u32[]{:S(2)}) collective-permute-start(f32[512,128]{0,1:T(8,128)S(1)} %fusion.25), channel_id=1, source_target_pairs={{0,8},{8,16},{16,24},{1,9},{9,17},{17,25},{2,10},{10,18},{18,26},{... | collective-permute-start | bytes 786440 | tf_op jit(solution)/shard_map/while/body/eval_jaxpr/ppermute | solution.py:10
  94.1 39.1 %reduce-scatter.5.cloned.1.call-start = ((), (), s32[]{:S(2)}) async-start(), calls=%async_computation.3 | async-start | bytes 589824 | tf_op jit(solution)/shard_map/while/body/eval_jaxpr/reduce_scatter | solution.py:46
  134.8 4.6 collective-permute-start
  139.3 4.4 collective-permute-start.1
  143.8 4.2 collective-permute-start.2
  148.0 4.2 collective-permute-start.3
  152.3 4.2 collective-permute-start.4
  156.5 4.2 collective-permute-start.5
  160.7 4.2 collective-permute-start.6
  166.7 7.3 %collective-permute-start.7 = (f32[512,128]{0,1:T(8,128)S(1)}, f32[512,128]{0,1:T(8,128)}, u32[]{:S(2)}, u32[]{:S(2)}) collective-permute-start(f32[512,128]{0,1:T(8,128)S(1)} %fusion.25), channel_id=1, source_target_pairs={{0,8},{8,16},{16,24},{1,9},{9,17},{17,25},{2,10},{10,18},{18,26},{... | collective-permute-start | bytes 786440 | tf_op jit(solution)/shard_map/while/body/eval_jaxpr/ppermute | solution.py:10
  174.0 39.1 %reduce-scatter.5.cloned.1.call-start = ((), (), s32[]{:S(2)}) async-start(), calls=%async_computation.3 | async-start | bytes 589824 | tf_op jit(solution)/shard_map/while/body/eval_jaxpr/reduce_scatter | solution.py:46
  214.6 4.6 collective-permute-start
  219.2 4.4 collective-permute-start.1
  223.6 4.2 collective-permute-start.2
  227.9 4.2 collective-permute-start.3
  232.1 4.2 collective-permute-start.4
  236.3 4.2 collective-permute-start.5
  240.6 4.2 collective-permute-start.6
  246.6 7.3 %collective-permute-start.7 = (f32[512,128]{0,1:T(8,128)S(1)}, f32[512,128]{0,1:T(8,128)}, u32[]{:S(2)}, u32[]{:S(2)}) collective-permute-start(f32[512,128]{0,1:T(8,128)S(1)} %fusion.25), channel_id=1, source_target_pairs={{0,8},{8,16},{16,24},{1,9},{9,17},{17,25},{2,10},{10,18},{18,26},{... | collective-permute-start | bytes 786440 | tf_op jit(solution)/shard_map/while/body/eval_jaxpr/ppermute | solution.py:10
  253.9 38.8 %reduce-scatter.5.cloned.1.call-start = ((), (), s32[]{:S(2)}) async-start(), calls=%async_computation.3 | async-start | bytes 589824 | tf_op jit(solution)/shard_map/while/body/eval_jaxpr/reduce_scatter | solution.py:46
  294.2 4.6 collective-permute-start
  298.7 4.4 collective-permute-start.1
  303.2 4.2 collective-permute-start.2
  307.4 4.2 collective-permute-start.3
  311.7 4.2 collective-permute-start.4
  315.9 4.2 collective-permute-start.5
  320.1 4.2 collective-permute-start.6
  326.1 7.3 %collective-permute-start.7 = (f32[512,128]{0,1:T(8,128)S(1)}, f32[512,128]{0,1:T(8,128)}, u32[]{:S(2)}, u32[]{:S(2)}) collective-permute-start(f32[512,128]{0,1:T(8,128)S(1)} %fusion.25), channel_id=1, source_target_pairs={{0,8},{8,16},{16,24},{1,9},{9,17},{17,25},{2,10},{10,18},{18,26},{... | collective-permute-start | bytes 786440 | tf_op jit(solution)/shard_map/while/body/eval_jaxpr/ppermute | solution.py:10
  333.4 38.8 %reduce-scatter.5.cloned.1.call-start = ((), (), s32[]{:S(2)}) async-start(), calls=%async_computation.3 | async-start | bytes 589824 | tf_op jit(solution)/shard_map/while/body/eval_jaxpr/reduce_scatter | solution.py:46
  373.7 4.6 collective-permute-start
  378.3 4.4 collective-permute-start.1
  382.7 4.2 collective-permute-start.2
  387.0 4.2 collective-permute-start.3
  391.2 4.2 collective-permute-start.4
  395.4 4.2 collective-permute-start.5
  399.7 4.2 collective-permute-start.6
  405.7 7.3 %collective-permute-start.7 = (f32[512,128]{0,1:T(8,128)S(1)}, f32[512,128]{0,1:T(8,128)}, u32[]{:S(2)}, u32[]{:S(2)}) collective-permute-start(f32[512,128]{0,1:T(8,128)S(1)} %fusion.25), channel_id=1, source_target_pairs={{0,8},{8,16},{16,24},{1,9},{9,17},{17,25},{2,10},{10,18},{18,26},{... | collective-permute-start | bytes 786440 | tf_op jit(solution)/shard_map/while/body/eval_jaxpr/ppermute | solution.py:10
  413.0 38.8 %reduce-scatter.5.cloned.1.call-start = ((), (), s32[]{:S(2)}) async-start(), calls=%async_computation.3 | async-start | bytes 589824 | tf_op jit(solution)/shard_map/while/body/eval_jaxpr/reduce_scatter | solution.py:46
  453.3 4.6 collective-permute-start
  457.8 4.4 collective-permute-start.1
  462.3 4.2 collective-permute-start.2
  466.5 4.2 collective-permute-start.3
  470.8 4.2 collective-permute-start.4
  475.0 4.2 collective-permute-start.5
  479.3 4.2 collective-permute-start.6
  485.3 7.3 %collective-permute-start.7 = (f32[512,128]{0,1:T(8,128)S(1)}, f32[512,128]{0,1:T(8,128)}, u32[]{:S(2)}, u32[]{:S(2)}) collective-permute-start(f32[512,128]{0,1:T(8,128)S(1)} %fusion.25), channel_id=1, source_target_pairs={{0,8},{8,16},{16,24},{1,9},{9,17},{17,25},{2,10},{10,18},{18,26},{... | collective-permute-start | bytes 786440 | tf_op jit(solution)/shard_map/while/body/eval_jaxpr/ppermute | solution.py:10
  492.6 39.1 %reduce-scatter.5.cloned.1.call-start = ((), (), s32[]{:S(2)}) async-start(), calls=%async_computation.3 | async-start | bytes 589824 | tf_op jit(solution)/shard_map/while/body/eval_jaxpr/reduce_scatter | solution.py:46
  533.2 4.6 collective-permute-start
  537.7 4.4 collective-permute-start.1
  542.2 4.2 collective-permute-start.2
  546.4 4.2 collective-permute-start.3
  550.7 4.2 collective-permute-start.4
  554.9 4.2 collective-permute-start.5
  559.1 4.2 collective-permute-start.6
  565.2 7.3 %collective-permute-start.7 = (f32[512,128]{0,1:T(8,128)S(1)}, f32[512,128]{0,1:T(8,128)}, u32[]{:S(2)}, u32[]{:S(2)}) collective-permute-start(f32[512,128]{0,1:T(8,128)S(1)} %fusion.25), channel_id=1, source_target_pairs={{0,8},{8,16},{16,24},{1,9},{9,17},{17,25},{2,10},{10,18},{18,26},{... | collective-permute-start | bytes 786440 | tf_op jit(solution)/shard_map/while/body/eval_jaxpr/ppermute | solution.py:10
  572.4 31.8 %reduce-scatter.3.cloned.1.call-start = ((), (), s32[]{:S(2)}) async-start(), calls=%async_computation.2 | async-start | bytes 1310720 | tf_op jit(solution)/shard_map/reduce_scatter | solution.py:83
  (9 other events, 257.9 us)
Sparse Core Ops, SparseCore 0:
  16.5 36.8 reduce-scatter.4
  98.0 35.2 reduce-scatter.4
  177.9 35.1 reduce-scatter.4
  257.4 35.1 reduce-scatter.4
  337.0 35.1 reduce-scatter.4
  416.5 35.2 reduce-scatter.4
  496.4 35.2 reduce-scatter.4
Sparse Core Ops, SparseCore 1:
  575.9 28.3 reduce-scatter.2
